TPU v7x, 128 devices: a whole 4x4x4 slice. The times are simulated.
128 devices in a mesh: src: 4 (over y), tgt: 32 (over x, z, core).
Axes of the slice: x: 4, y: 4, z: 4, core: 2. Of those that a mesh axis runs over, the one named last changes fastest.
Arguments:
- source_pca: float32 [64, 16384], P(None, 'src'), may hold values from -6 to 6
- target_pca: float32 [64, 32768], P(None, 'tgt'), may hold values from -6 to 6
- source_labels: int32 [16384], P('src'), may hold values from 0 to 63, as said below
- target_labels: int32 [32768], P('tgt'), may hold values from 0 to 63, as said below
- block_mask: int32 [64, 64], replicated, may hold values from 0 to 1, as said below
Outputs:
- source_projection: float32 [64, 16384], P(None, ('src', 'tgt'))
- target_projection: float32 [64, 32768], P(None, 'tgt')
Inputs may be any that keep to these rules, and one draw needn't show every extreme that they name: `source_labels`: each aligned block of 4096 consecutive source cells holds every one of the 64 clusters. `target_labels`: each aligned block of 1024 consecutive target cells holds every one of the 64 clusters. `block_mask`: entries are 0 or 1, and the diagonal is all ones.
All inputs are finite; a program needn't handle non-finite values.
Results may differ from a plain program's by a relative error of at most 0.0003.
Values sent between devices are 32-bit elements; how exact they have to be, the bound alone decides.
A program may use at most 64 MiB of HBM per device.

v0:
```python
import functools
import math

import jax
import jax.numpy as jnp
from jax import lax
from jax.experimental import pallas as pl
from jax.experimental.pallas import tpu as pltpu
from jax.sharding import PartitionSpec as P

ITERS = 2
EPSILON = 0.05
BARRED = -(2.0**100)
MESH = pl.DeviceIdType.MESH
F32 = jnp.float32
BF16 = jnp.bfloat16
LANES = 128
GROUP = 8
PAD = 72


def in_three(value):
    first = value.astype(BF16)
    rest = value - first.astype(F32)
    second = rest.astype(BF16)
    third = (rest - second.astype(F32)).astype(BF16)
    return first, second, third


def in_two(value):
    first = value.astype(BF16)
    return first, (value - first.astype(F32)).astype(BF16)


def turned(row):
    return jnp.broadcast_to(row, (LANES, LANES)).T


def lse_of(parts):
    top = functools.reduce(jnp.maximum, parts)
    return top + jnp.log2(sum(jnp.exp2(p - top) for p in parts))


def span(index, size):
    return pl.ds(pl.multiple_of(index * size, size), size)


def kernel(S, T, x_ref, y_ref, sl_ref, tl_ref, mask_ref, so_ref, to_ref,
           xa, ya, zr, ehi, elo, frow, mp, mb, sp, sb, xw, yw,
           lbuf, lrec, lpair, lprec, mbuf, gbuf, grec,
           rbuf, rrec, rpair, rprec, cbuf, crec,
           wbuf, wrec, tbuf, trec, sbuf, prec, pbuf, srec,
           lsend, lrecv, psend, precv, gsend, grecv,
           rsend, rrecv, qsend, qrecv, csend, crecv,
           wsend, wrecv, tsend, trecv, bsend, brecv, ssend, srecv):
    dims, R = x_ref.shape
    C = y_ref.shape[1]
    G = T // 2
    QW = C // S
    CB = C // LANES
    RB = R // LANES
    scale = math.log2(math.e) / (EPSILON * dims)
    me_s, me_t = lax.axis_index("src"), lax.axis_index("tgt")
    core = lax.rem(me_t, 2)
    chip = me_t // 2
    partner = me_t + 1 - 2 * core

    def mate(o):
        return (me_s, lax.rem(me_t + 2 * o, T))

    def above(o):
        return (lax.rem(me_s + o, S), me_t)

    pair = (me_s, partner)
    everyone = [mate(o) for o in range(1, G)] + [above(o) for o in range(1, S)] + [pair]
    barrier = pltpu.get_barrier_semaphore()
    for device in everyone:
        pl.semaphore_signal(barrier, inc=1, device_id=device, device_id_type=MESH)

    def remote(src, dst, send, recv, device):
        return pltpu.make_async_remote_copy(
            src_ref=src, dst_ref=dst, send_sem=send, recv_sem=recv,
            device_id=device, device_id_type=MESH)

    def to_mates(src, dst, send, recv):
        return [remote(src, dst.at[o - 1], send.at[o - 1], recv.at[o - 1], mate(o))
                for o in range(1, G)]

    def to_column(src, dst, send, recv):
        return [remote(src, dst.at[o - 1], send.at[o - 1], recv.at[o - 1], above(o))
                for o in range(1, S)]

    def begin(copies):
        for copy in copies:
            copy.start()

    def finish(copies):
        for copy in copies:
            copy.wait()

    XC = 512

    def prepare_source(c, _):
        at = span(c, XC)
        x = x_ref[:, at]
        x1, x2, x3 = in_three(x)
        for k, part in enumerate((x1, x2, x1, x2, x3, x1)):
            xa[k * dims:(k + 1) * dims, at] = part
        ids = lax.broadcasted_iota(jnp.int32, (dims, XC), 0)
        xa[6 * dims:7 * dims, at] = jnp.where(ids == sl_ref[:, at], 1.0, 0.0).astype(BF16)
        n1, n2, n3 = (p.astype(F32) for p in in_three(-scale * jnp.sum(x * x, 0, keepdims=True)))
        norm = jnp.where(ids == 3, n1, jnp.where(ids == 4, n2, jnp.where(ids == 5, n3, 0.0)))
        xa[7 * dims:8 * dims, at] = jnp.where(ids < 3, 1.0, norm).astype(BF16)
        return 0

    lax.fori_loop(0, R // XC, prepare_source, 0)

    y = y_ref[...]
    y1, y2, y3 = (p.astype(F32) for p in in_three(2.0 * scale * y))
    ids = lax.broadcasted_iota(jnp.int32, (dims, C), 0)
    onehot = jnp.where(ids == tl_ref[...], 1.0, 0.0).astype(BF16)
    allowed = jnp.dot(mask_ref[...].astype(F32).astype(BF16), onehot, preferred_element_type=F32)
    penalty = jnp.where(allowed > 0.5, 0.0, BARRED)
    n1, n2, n3 = (p.astype(F32) for p in in_three(-scale * jnp.sum(y * y, 0, keepdims=True)))
    norm = jnp.where(ids == 0, n1, jnp.where(ids == 1, n2, jnp.where(ids == 2, n3, 0.0)))
    norm = jnp.where((ids >= 3) & (ids < 6), 1.0, norm)
    for k, (a, b) in enumerate(((y1, y1), (y2, y2), (y1, y3), (penalty, norm))):
        ya[:, k * LANES:(k + 1) * LANES] = jnp.concatenate([a, b], 0).T.astype(BF16)

    def first_rows(i, _):
        at = span(i, 2 * LANES)
        z = jnp.dot(ya[...], xa[:, at], preferred_element_type=F32)
        zr[:, at] = z
        top = jnp.max(z, 0, keepdims=True)
        lse = top + jnp.log2(jnp.sum(jnp.exp2(z - top), 0, keepdims=True))
        lbuf[pl.ds(2 * i, 1), :] = lse[:, :LANES]
        lbuf[pl.ds(2 * i + 1, 1), :] = lse[:, LANES:]
        return 0

    lax.fori_loop(0, R // (2 * LANES), first_rows, 0)

    pl.semaphore_wait(barrier, len(everyone))
    copies = to_mates(lbuf, lrec, lsend, lrecv)
    begin(copies)
    finish(copies)
    lpair[...] = lse_of([lbuf[...]] + [lrec[o] for o in range(G - 1)])
    copy = remote(lpair, lprec, psend, precv, pair)
    copy.start()
    copy.wait()
    f = -math.log2(R * S) - lse_of([lpair[...], lprec[...]])
    for q in range(RB):
        frow[:, q * LANES:(q + 1) * LANES] = jnp.broadcast_to(f[q:q + 1, :], (GROUP, LANES))

    def chunks(q):
        return slice(q * LANES, (q + 1) * LANES)

    def peaks(j, _):
        at = span(j, GROUP)
        mp[at, :] = functools.reduce(
            jnp.maximum, [zr[at, chunks(q)] + frow[:, chunks(q)] for q in range(RB)])
        return 0

    lax.fori_loop(0, C // GROUP, peaks, 0)
    for b in range(CB):
        rows = slice(b * LANES, (b + 1) * LANES)
        top = jnp.max(mp[rows, :].T, 0, keepdims=True)
        mbuf[b:b + 1, :] = top
        mb[rows, :] = turned(top)

    def weigh(j, _):
        at = span(j, GROUP)
        peak = mb[at, :]
        total = None
        for q in range(RB):
            e = jnp.exp2(zr[at, chunks(q)] + frow[:, chunks(q)] - peak)
            zr[at, chunks(q)] = e
            total = e if total is None else total + e
        sp[at, :] = total
        return 0

    lax.fori_loop(0, C // GROUP, weigh, 0)
    for b in range(CB):
        rows = slice(b * LANES, (b + 1) * LANES)
        total = jnp.sum(sp[rows, :].T, 0, keepdims=True)
        gbuf[b:b + 1, :] = mbuf[b:b + 1, :] + jnp.log2(total)

    copies = to_column(gbuf, grec, gsend, grecv)
    begin(copies)

    def halve(j, _):
        at = span(j, 2 * GROUP)
        ehi[at, :], elo[at, :] = in_two(zr[at, :])
        return 0

    lax.fori_loop(0, C // (2 * GROUP), halve, 0)
    finish(copies)
    lse = lse_of([gbuf[...]] + [grec[o] for o in range(S - 1)])
    sig = jnp.exp2(mbuf[...] - lse)
    mbuf[...] = sig
    for b in range(CB):
        sb[b * LANES:(b + 1) * LANES, :] = turned(sig[b:b + 1, :])

    RC = min(2048, R)
    for h in range(R // RC):

        def mass(j, acc):
            at = span(j, GROUP)
            weight = sb[at, :]
            return tuple(
                acc[q] + zr[at, h * RC + q * LANES:h * RC + (q + 1) * LANES] * weight
                for q in range(RC // LANES))

        acc = lax.fori_loop(
            0, C // GROUP, mass,
            tuple(jnp.zeros((GROUP, LANES), F32) for q in range(RC // LANES)))
        for q, part in enumerate(acc):
            at = h * (RC // LANES) + q
            rbuf[at:at + 1, :] = jnp.sum(part, 0, keepdims=True)

    copies = to_mates(rbuf, rrec, rsend, rrecv)
    begin(copies)
    finish(copies)
    rpair[...] = rbuf[...] + sum(rrec[o] for o in range(G - 1))
    copy = remote(rpair, rprec, qsend, qrecv, pair)
    copy.start()
    copy.wait()
    a = (C * T / (R * S)) / (rpair[...] + rprec[...])
    for q in range(RB):
        frow[:, chunks(q)] = jnp.broadcast_to(a[q:q + 1, :], (GROUP, LANES))

    def sums(j, _):
        at = span(j, GROUP)
        total = None
        for q in range(RB):
            e = zr[at, chunks(q)] * frow[:, chunks(q)]
            total = e if total is None else total + e
        sp[at, :] = total
        return 0

    lax.fori_loop(0, C // GROUP, sums, 0)
    for b in range(CB):
        rows = slice(b * LANES, (b + 1) * LANES)
        cbuf[b:b + 1, :] = sig[b:b + 1, :] * jnp.sum(sp[rows, :].T, 0, keepdims=True)
    copies = to_column(cbuf, crec, csend, crecv)
    begin(copies)

    tail = lax.broadcasted_iota(jnp.int32, (2 * GROUP, LANES), 0)

    def with_mass(dst, at, value, mass):
        hi, lo = in_two(value)
        dst[0:dims, at] = hi
        dst[dims:2 * dims, at] = lo
        m1, m2 = (p.astype(F32) for p in in_two(mass))
        dst[2 * dims:2 * dims + 2 * GROUP, at] = jnp.where(
            tail == 0, m1, jnp.where(tail == 1, m2, 0.0)).astype(BF16)

    for q in range(RB):
        with_mass(xw, chunks(q), x_ref[:, chunks(q)] * a[q:q + 1, :], a[q:q + 1, :])

    def folded(out):
        value = out[0:dims] + out[dims:2 * dims]
        mass = jnp.sum(out[2 * dims:], 0, keepdims=True)
        return value, mass

    across = (((1,), (1,)), ((), ()))

    def target_sums(k, _):
        at = span(k, QW)
        value, mass = folded(
            lax.dot_general(xw[...], ehi[at, :], across, preferred_element_type=F32)
            + lax.dot_general(xw[...], elo[at, :], across, preferred_element_type=F32))
        for b in range(QW // LANES):
            row = mbuf[pl.ds(k * (QW // LANES) + b, 1), :]
            wbuf[k, 0:dims, chunks(b)] = value[:, chunks(b)] * row
            wbuf[k, dims:PAD, chunks(b)] = jnp.broadcast_to(
                mass[:, chunks(b)] * row, (PAD - dims, LANES))
        return 0

    lax.fori_loop(0, S, target_sums, 0)
    wcopies = [
        remote(wbuf.at[lax.rem(me_s + o, S)], wrec.at[o - 1], wsend.at[o - 1], wrecv.at[o - 1],
               above(o)) for o in range(1, S)]
    begin(wcopies)
    finish(copies)
    factor = sig / (cbuf[...] + sum(crec[o] for o in range(S - 1)))
    for b in range(CB):
        row = factor[b:b + 1, :]
        with_mass(yw, chunks(b), y_ref[:, chunks(b)] * row, row)

    def to_partner(o):
        return remote(sbuf.at[o, 1 - core], prec.at[o], bsend.at[o], brecv.at[o], pair)

    def to_owner(o):
        return remote(pbuf.at[o], srec.at[o - 1], ssend.at[o - 1], srecv.at[o - 1], mate(o))

    def source_sums(o):
        at = span(lax.rem(chip + o, G), 2 * LANES)
        value, mass = folded(
            jnp.dot(yw[...], ehi[:, at], preferred_element_type=F32)
            + jnp.dot(yw[...], elo[:, at], preferred_element_type=F32))
        for k in range(2):
            sbuf[o, k, 0:dims, :] = value[:, chunks(k)]
            sbuf[o, k, dims:PAD, :] = jnp.broadcast_to(mass[:, chunks(k)], (PAD - dims, LANES))
        to_partner(o).start()

    def pass_on(o):
        to_partner(o).wait_recv()
        pbuf[o] = sbuf[o, core] + prec[o]

    source_sums(1)

    def source_step(o, _):
        source_sums(lax.rem(o + 1, G))
        pass_on(o)
        to_owner(o).start()
        return 0

    lax.fori_loop(1, G, source_step, 0)
    pass_on(0)

    finish(wcopies)
    total = wbuf[me_s] + sum(wrec[o] for o in range(S - 1))
    tbuf[...] = total[0:dims] / total[dims:dims + 1]
    tcopies = to_column(tbuf, trec, tsend, trecv)
    begin(tcopies)
    to_ref[:, span(me_s, QW)] = tbuf[...]

    def settle(o, acc):
        to_owner(o).wait()
        return acc + srec[o - 1]

    total = lax.fori_loop(1, G, settle, pbuf[0])
    so_ref[...] = total[0:dims] / total[dims:dims + 1]

    def sent(o, _):
        to_partner(o).wait_send()
        return 0

    lax.fori_loop(0, G, sent, 0)
    finish(tcopies)
    for o in range(1, S):
        to_ref[:, span(lax.rem(me_s + S - o, S), QW)] = trec[o - 1]


def shards(S, T, source_pca, target_pca, source_labels, target_labels, block_mask):
    dims, R = source_pca.shape
    C = target_pca.shape[1]
    G = T // 2
    CB, RB = C // LANES, R // LANES
    vmem = pltpu.VMEM
    dma = pltpu.SemaphoreType.DMA
    whole = pl.BlockSpec(memory_space=pltpu.VMEM)
    return pl.pallas_call(
        functools.partial(kernel, S, T),
        out_shape=(jax.ShapeDtypeStruct((dims, R // T), F32), jax.ShapeDtypeStruct((dims, C), F32)),
        in_specs=[whole] * 5,
        out_specs=(whole, whole),
        scratch_shapes=[
            vmem((8 * dims, R), BF16), vmem((C, 8 * dims), BF16), vmem((C, R), F32),
            vmem((C, R), BF16), vmem((C, R), BF16), vmem((GROUP, R), F32),
            vmem((C, LANES), F32), vmem((C, LANES), F32), vmem((C, LANES), F32),
            vmem((C, LANES), F32),
            vmem((2 * dims + 2 * GROUP, R), BF16), vmem((2 * dims + 2 * GROUP, C), BF16),
            vmem((RB, LANES), F32), vmem((G - 1, RB, LANES), F32), vmem((RB, LANES), F32),
            vmem((RB, LANES), F32),
            vmem((CB, LANES), F32), vmem((CB, LANES), F32), vmem((S - 1, CB, LANES), F32),
            vmem((RB, LANES), F32), vmem((G - 1, RB, LANES), F32), vmem((RB, LANES), F32),
            vmem((RB, LANES), F32),
            vmem((CB, LANES), F32), vmem((S - 1, CB, LANES), F32),
            vmem((S, PAD, C // S), F32), vmem((S - 1, PAD, C // S), F32),
            vmem((dims, C // S), F32), vmem((S - 1, dims, C // S), F32),
            vmem((G, 2, PAD, LANES), F32), vmem((G, PAD, LANES), F32), vmem((G, PAD, LANES), F32),
            vmem((G - 1, PAD, LANES), F32),
            dma((G - 1,)), dma((G - 1,)), dma, dma, dma((S - 1,)), dma((S - 1,)),
            dma((G - 1,)), dma((G - 1,)), dma, dma, dma((S - 1,)), dma((S - 1,)),
            dma((S - 1,)), dma((S - 1,)), dma((S - 1,)), dma((S - 1,)),
            dma((G,)), dma((G,)), dma((G - 1,)), dma((G - 1,)),
        ],
        compiler_params=pltpu.CompilerParams(
            collective_id=0, has_side_effects=True, vmem_limit_bytes=60 * 2**20),
    )(source_pca, target_pca, source_labels.reshape(1, R), target_labels.reshape(1, C), block_mask)


def solution(mesh):
    placed = (P(None, "src"), P(None, "tgt"), P("src"), P("tgt"), P())
    return jax.shard_map(
        functools.partial(shards, mesh.shape["src"], mesh.shape["tgt"]),
        mesh=mesh,
        in_specs=placed,
        out_specs=(P(None, ("src", "tgt")), P(None, "tgt")),
        check_vma=False,
    )
```

profile of v0, /device:TPU:1, one launch (start us, length us, event | category | flops | bytes accessed | tf_op | source)
XLA Modules:
  0.0 84.2 jit_solution(7947285327347600414)
XLA Ops:
  0.6 80.5 %shard_map.68 = (f32[64,128]{1,0:T(8,128)}, f32[64,1024]{1,0:T(8,128)}) custom-call(f32[64,4096]{1,0:T(8,128)} %x_ref.1, f32[64,1024]{1,0:T(8,128)} %y_ref.1, s32[1,4096]{1,0:T(1,128)} %bitcast.2, s32[1,1024]{1,0:T(1,128)} %bitcast.3, s32[64,64]{1,0:T(8,128)} %mask_ref.1), custom_call_target="tpu_custom_call" | custom-call | tf_op jit(solution)/shard_map/pallas_call | solution.py:353
  81.2 1.4 %copy.9 = f32[64,128]{1,0:T(8,128)} copy(f32[64,128]{1,0:T(8,128)} %get-tuple-element.4) | data formatting | bytes 65536
  82.5 1.7 %copy.10 = f32[64,1024]{1,0:T(8,128)} copy(f32[64,1024]{1,0:T(8,128)} %get-tuple-element.5) | data formatting | bytes 524288
where the time goes:
time: 84.4 us; the launch traced here: 84.2 us
  Pallas kernels  80.5 us (95%)
  local copies, waits for them, and re-layouts  3.05 us (4%)
    pallas_call x1, Pallas kernels, shards(): pl.pallas_call(functools.partial(kernel, S, T), out_shape=(jax.ShapeDtype...  80.5 us
    unnamed x2, local copies, waits for them, and re-layouts  3.05 us

commit v1 on v0

--- a/solution.py
+++ b/solution.py
@@ -47,8 +47,8 @@
 
 def kernel(S, T, x_ref, y_ref, sl_ref, tl_ref, mask_ref, so_ref, to_ref,
            xa, ya, zr, ehi, elo, frow, mp, mb, sp, sb, xw, yw,
-           lbuf, lrec, lpair, lprec, mbuf, gbuf, grec,
-           rbuf, rrec, rpair, rprec, cbuf, crec,
+           lbuf, lrec, lpair, lown, lprec, mbuf, gbuf, grec,
+           rbuf, rrec, rpair, rown, rprec, cbuf, crec,
            wbuf, wrec, tbuf, trec, sbuf, prec, pbuf, srec,
            lsend, lrecv, psend, precv, gsend, grecv,
            rsend, rrecv, qsend, qrecv, csend, crecv,
@@ -98,16 +98,27 @@
         for copy in copies:
             copy.wait()
 
-    XC = 512
+    def chunks(q):
+        return slice(q * LANES, (q + 1) * LANES)
+
+    XC = min(512, R // 2)
+
+    half = R // 2
+    half_rows = RB // 2
+
+    def natural(slot):
+        return slot + core - 2 * slot * core
 
     def prepare_source(c, _):
         at = span(c, XC)
-        x = x_ref[:, at]
+        place = natural(c // (half // XC)) * half + lax.rem(c, half // XC) * XC
+        place = pl.ds(pl.multiple_of(place, XC), XC)
+        x = x_ref[:, place]
         x1, x2, x3 = in_three(x)
         for k, part in enumerate((x1, x2, x1, x2, x3, x1)):
             xa[k * dims:(k + 1) * dims, at] = part
         ids = lax.broadcasted_iota(jnp.int32, (dims, XC), 0)
-        xa[6 * dims:7 * dims, at] = jnp.where(ids == sl_ref[:, at], 1.0, 0.0).astype(BF16)
+        xa[6 * dims:7 * dims, at] = jnp.where(ids == sl_ref[:, place], 1.0, 0.0).astype(BF16)
         n1, n2, n3 = (p.astype(F32) for p in in_three(-scale * jnp.sum(x * x, 0, keepdims=True)))
         norm = jnp.where(ids == 3, n1, jnp.where(ids == 4, n2, jnp.where(ids == 5, n3, 0.0)))
         xa[7 * dims:8 * dims, at] = jnp.where(ids < 3, 1.0, norm).astype(BF16)
@@ -127,40 +138,78 @@
     for k, (a, b) in enumerate(((y1, y1), (y2, y2), (y1, y3), (penalty, norm))):
         ya[:, k * LANES:(k + 1) * LANES] = jnp.concatenate([a, b], 0).T.astype(BF16)
 
-    def first_rows(i, _):
-        at = span(i, 2 * LANES)
-        z = jnp.dot(ya[...], xa[:, at], preferred_element_type=F32)
-        zr[:, at] = z
-        top = jnp.max(z, 0, keepdims=True)
-        lse = top + jnp.log2(jnp.sum(jnp.exp2(z - top), 0, keepdims=True))
-        lbuf[pl.ds(2 * i, 1), :] = lse[:, :LANES]
-        lbuf[pl.ds(2 * i + 1, 1), :] = lse[:, LANES:]
-        return 0
-
-    lax.fori_loop(0, R // (2 * LANES), first_rows, 0)
-
+    block = 2 * LANES
+    sub = 8 * GROUP
+
+    def first_rows(slot):
+        behind = None
+        for u in range(half // block + 1):
+            ahead = None
+            if u < half // block:
+                at = slice(slot * half + u * block, slot * half + (u + 1) * block)
+                z = jnp.dot(ya[...], xa[:, at], preferred_element_type=F32)
+                zr[:, at] = z
+                tops = functools.reduce(
+                    jnp.maximum, [z[k * sub:(k + 1) * sub] for k in range(C // sub)])
+                ahead = at, jnp.max(tops, 0, keepdims=True)
+            if behind is not None:
+                at, top = behind
+                total = sum(
+                    jnp.exp2(zr[k * sub:(k + 1) * sub, at] - top) for k in range(C // sub))
+                lse = top + jnp.log2(jnp.sum(total, 0, keepdims=True))
+                for k in range(2):
+                    lbuf[slot, 2 * (u - 1) + k:2 * (u - 1) + k + 1, :] = lse[:, chunks(k)]
+            behind = ahead
+
+    first_rows(1)
     pl.semaphore_wait(barrier, len(everyone))
-    copies = to_mates(lbuf, lrec, lsend, lrecv)
+    early = remote(lbuf.at[1], lprec.at[0], psend.at[0], precv.at[0], pair)
+    early.start()
+    first_rows(0)
+    early.wait()
+    lpair[...] = lse_of([lbuf[0], lprec[0]])
+    copies = to_mates(lpair, lrec, lsend, lrecv)
     begin(copies)
     finish(copies)
-    lpair[...] = lse_of([lbuf[...]] + [lrec[o] for o in range(G - 1)])
-    copy = remote(lpair, lprec, psend, precv, pair)
-    copy.start()
-    copy.wait()
-    f = -math.log2(R * S) - lse_of([lpair[...], lprec[...]])
-    for q in range(RB):
-        frow[:, q * LANES:(q + 1) * LANES] = jnp.broadcast_to(f[q:q + 1, :], (GROUP, LANES))
-
-    def chunks(q):
-        return slice(q * LANES, (q + 1) * LANES)
-
-    def peaks(j, _):
-        at = span(j, GROUP)
-        mp[at, :] = functools.reduce(
-            jnp.maximum, [zr[at, chunks(q)] + frow[:, chunks(q)] for q in range(RB)])
-        return 0
-
-    lax.fori_loop(0, C // GROUP, peaks, 0)
+    lown[...] = -math.log2(R * S) - lse_of([lpair[...]] + [lrec[o] for o in range(G - 1)])
+    late = remote(lown, lprec.at[1], psend.at[1], precv.at[1], pair)
+    late.start()
+
+    def lanes_of(slot, q):
+        return slice(slot * half + q * LANES, slot * half + (q + 1) * LANES)
+
+    def spread(slot, value):
+        for q in range(half_rows):
+            frow[:, lanes_of(slot, q)] = jnp.broadcast_to(value[q:q + 1, :], (GROUP, LANES))
+
+    WIDE = 4
+
+    def parts_of(value):
+        return [value[g * GROUP:(g + 1) * GROUP] for g in range(value.shape[0] // GROUP)]
+
+    def by_rows(slot, step, combine, into, more):
+
+        def body(j, _):
+            at = span(j, WIDE * GROUP)
+            acc = [[None, None] for _ in range(WIDE)]
+            for q in range(half_rows):
+                row = frow[:, lanes_of(slot, q)]
+                for g, z in enumerate(parts_of(zr[at, lanes_of(slot, q)])):
+                    value = step(z, row)
+                    old = acc[g][q % 2]
+                    acc[g][q % 2] = value if old is None else combine(old, value)
+            value = jnp.concatenate([combine(*pair_) for pair_ in acc], 0)
+            into[at, :] = combine(into[at, :], value) if more else value
+            return 0
+
+        lax.fori_loop(0, C // (WIDE * GROUP), body, 0)
+
+    spread(0, lown[...])
+    by_rows(0, jnp.add, jnp.maximum, mp, False)
+    late.wait()
+    spread(1, lprec[1])
+    by_rows(1, jnp.add, jnp.maximum, mp, True)
+
     for b in range(CB):
         rows = slice(b * LANES, (b + 1) * LANES)
         top = jnp.max(mp[rows, :].T, 0, keepdims=True)
@@ -168,17 +217,18 @@
         mb[rows, :] = turned(top)
 
     def weigh(j, _):
-        at = span(j, GROUP)
+        at = span(j, 2 * GROUP)
         peak = mb[at, :]
-        total = None
+        acc = [None, None]
         for q in range(RB):
-            e = jnp.exp2(zr[at, chunks(q)] + frow[:, chunks(q)] - peak)
+            row = jnp.concatenate([frow[:, chunks(q)]] * 2, 0)
+            e = jnp.exp2(zr[at, chunks(q)] + row - peak)
             zr[at, chunks(q)] = e
-            total = e if total is None else total + e
-        sp[at, :] = total
+            acc[q % 2] = e if acc[q % 2] is None else acc[q % 2] + e
+        sp[at, :] = acc[0] + acc[1]
         return 0
 
-    lax.fori_loop(0, C // GROUP, weigh, 0)
+    lax.fori_loop(0, C // (2 * GROUP), weigh, 0)
     for b in range(CB):
         rows = slice(b * LANES, (b + 1) * LANES)
         total = jnp.sum(sp[rows, :].T, 0, keepdims=True)
@@ -196,48 +246,42 @@
     finish(copies)
     lse = lse_of([gbuf[...]] + [grec[o] for o in range(S - 1)])
     sig = jnp.exp2(mbuf[...] - lse)
-    mbuf[...] = sig
     for b in range(CB):
         sb[b * LANES:(b + 1) * LANES, :] = turned(sig[b:b + 1, :])
 
-    RC = min(2048, R)
-    for h in range(R // RC):
-
-        def mass(j, acc):
-            at = span(j, GROUP)
-            weight = sb[at, :]
-            return tuple(
-                acc[q] + zr[at, h * RC + q * LANES:h * RC + (q + 1) * LANES] * weight
-                for q in range(RC // LANES))
-
-        acc = lax.fori_loop(
-            0, C // GROUP, mass,
-            tuple(jnp.zeros((GROUP, LANES), F32) for q in range(RC // LANES)))
+    def row_mass(slot):
+
+        def body(j, acc):
+            at = span(j, WIDE * GROUP)
+            acc = list(acc)
+            weights = parts_of(sb[at, :])
+            for q in range(half_rows):
+                terms = [z * w for z, w in zip(parts_of(zr[at, lanes_of(slot, q)]), weights)]
+                acc[q] = acc[q] + ((terms[0] + terms[1]) + (terms[2] + terms[3]))
+            return tuple(acc)
+
+        zero = jnp.zeros((GROUP, LANES), F32)
+        acc = lax.fori_loop(0, C // (WIDE * GROUP), body, (zero,) * half_rows)
         for q, part in enumerate(acc):
-            at = h * (RC // LANES) + q
-            rbuf[at:at + 1, :] = jnp.sum(part, 0, keepdims=True)
-
-    copies = to_mates(rbuf, rrec, rsend, rrecv)
+            rbuf[slot, q:q + 1, :] = jnp.sum(part, 0, keepdims=True)
+
+    row_mass(1)
+    early = remote(rbuf.at[1], rprec.at[0], qsend.at[0], qrecv.at[0], pair)
+    early.start()
+    row_mass(0)
+    early.wait()
+    rpair[...] = rbuf[0] + rprec[0]
+    copies = to_mates(rpair, rrec, rsend, rrecv)
     begin(copies)
     finish(copies)
-    rpair[...] = rbuf[...] + sum(rrec[o] for o in range(G - 1))
-    copy = remote(rpair, rprec, qsend, qrecv, pair)
-    copy.start()
-    copy.wait()
-    a = (C * T / (R * S)) / (rpair[...] + rprec[...])
-    for q in range(RB):
-        frow[:, chunks(q)] = jnp.broadcast_to(a[q:q + 1, :], (GROUP, LANES))
-
-    def sums(j, _):
-        at = span(j, GROUP)
-        total = None
-        for q in range(RB):
-            e = zr[at, chunks(q)] * frow[:, chunks(q)]
-            total = e if total is None else total + e
-        sp[at, :] = total
-        return 0
-
-    lax.fori_loop(0, C // GROUP, sums, 0)
+    rown[...] = (C * T / (R * S)) / (rpair[...] + sum(rrec[o] for o in range(G - 1)))
+    late = remote(rown, rprec.at[1], qsend.at[1], qrecv.at[1], pair)
+    late.start()
+    spread(0, rown[...])
+    by_rows(0, jnp.multiply, jnp.add, sp, False)
+    late.wait()
+    spread(1, rprec[1])
+    by_rows(1, jnp.multiply, jnp.add, sp, True)
     for b in range(CB):
         rows = slice(b * LANES, (b + 1) * LANES)
         cbuf[b:b + 1, :] = sig[b:b + 1, :] * jnp.sum(sp[rows, :].T, 0, keepdims=True)
@@ -255,7 +299,10 @@
             tail == 0, m1, jnp.where(tail == 1, m2, 0.0)).astype(BF16)
 
     for q in range(RB):
-        with_mass(xw, chunks(q), x_ref[:, chunks(q)] * a[q:q + 1, :], a[q:q + 1, :])
+        row = frow[0:1, chunks(q)]
+        place = natural(q // half_rows) * half + (q % half_rows) * LANES
+        place = pl.ds(pl.multiple_of(place, LANES), LANES)
+        with_mass(xw, chunks(q), x_ref[:, place] * row, row)
 
     def folded(out):
         value = out[0:dims] + out[dims:2 * dims]
@@ -264,19 +311,16 @@
 
     across = (((1,), (1,)), ((), ()))
 
-    def target_sums(k, _):
-        at = span(k, QW)
+    for k in range(S):
+        at = slice(k * QW, (k + 1) * QW)
         value, mass = folded(
             lax.dot_general(xw[...], ehi[at, :], across, preferred_element_type=F32)
             + lax.dot_general(xw[...], elo[at, :], across, preferred_element_type=F32))
         for b in range(QW // LANES):
-            row = mbuf[pl.ds(k * (QW // LANES) + b, 1), :]
+            row = sig[k * (QW // LANES) + b:k * (QW // LANES) + b + 1, :]
             wbuf[k, 0:dims, chunks(b)] = value[:, chunks(b)] * row
             wbuf[k, dims:PAD, chunks(b)] = jnp.broadcast_to(
                 mass[:, chunks(b)] * row, (PAD - dims, LANES))
-        return 0
-
-    lax.fori_loop(0, S, target_sums, 0)
     wcopies = [
         remote(wbuf.at[lax.rem(me_s + o, S)], wrec.at[o - 1], wsend.at[o - 1], wrecv.at[o - 1],
                above(o)) for o in range(1, S)]
@@ -294,28 +338,44 @@
         return remote(pbuf.at[o], srec.at[o - 1], ssend.at[o - 1], srecv.at[o - 1], mate(o))
 
     def source_sums(o):
-        at = span(lax.rem(chip + o, G), 2 * LANES)
+        owner = lax.rem(chip + o, G)
+        place = natural(owner // (G // 2)) * half + lax.rem(owner, G // 2) * (2 * LANES)
+        at = pl.ds(pl.multiple_of(place, 2 * LANES), 2 * LANES)
         value, mass = folded(
             jnp.dot(yw[...], ehi[:, at], preferred_element_type=F32)
             + jnp.dot(yw[...], elo[:, at], preferred_element_type=F32))
         for k in range(2):
             sbuf[o, k, 0:dims, :] = value[:, chunks(k)]
             sbuf[o, k, dims:PAD, :] = jnp.broadcast_to(mass[:, chunks(k)], (PAD - dims, LANES))
-        to_partner(o).start()
 
     def pass_on(o):
         to_partner(o).wait_recv()
         pbuf[o] = sbuf[o, core] + prec[o]
 
-    source_sums(1)
-
-    def source_step(o, _):
-        source_sums(lax.rem(o + 1, G))
-        pass_on(o)
-        to_owner(o).start()
+    V = min(4, G)
+
+    def compute(g):
+        for v in range(V):
+            source_sums(lax.rem(g * V + v + 1, G))
+        for v in range(V):
+            to_partner(lax.rem(g * V + v + 1, G)).start()
+
+    def relay(g):
+        for v in range(V):
+            pass_on(g * V + v + 1)
+            to_owner(g * V + v + 1).start()
+
+    compute(0)
+
+    def source_step(g, _):
+        compute(g + 1)
+        relay(g)
         return 0
 
-    lax.fori_loop(1, G, source_step, 0)
+    lax.fori_loop(0, G // V - 1, source_step, 0)
+    for v in range(G - V + 1, G):
+        pass_on(v)
+        to_owner(v).start()
     pass_on(0)
 
     finish(wcopies)
@@ -361,18 +421,18 @@
             vmem((C, LANES), F32), vmem((C, LANES), F32), vmem((C, LANES), F32),
             vmem((C, LANES), F32),
             vmem((2 * dims + 2 * GROUP, R), BF16), vmem((2 * dims + 2 * GROUP, C), BF16),
-            vmem((RB, LANES), F32), vmem((G - 1, RB, LANES), F32), vmem((RB, LANES), F32),
-            vmem((RB, LANES), F32),
+            vmem((2, RB // 2, LANES), F32), vmem((G - 1, RB // 2, LANES), F32),
+            vmem((RB // 2, LANES), F32), vmem((RB // 2, LANES), F32), vmem((2, RB // 2, LANES), F32),
             vmem((CB, LANES), F32), vmem((CB, LANES), F32), vmem((S - 1, CB, LANES), F32),
-            vmem((RB, LANES), F32), vmem((G - 1, RB, LANES), F32), vmem((RB, LANES), F32),
-            vmem((RB, LANES), F32),
+            vmem((2, RB // 2, LANES), F32), vmem((G - 1, RB // 2, LANES), F32),
+            vmem((RB // 2, LANES), F32), vmem((RB // 2, LANES), F32), vmem((2, RB // 2, LANES), F32),
             vmem((CB, LANES), F32), vmem((S - 1, CB, LANES), F32),
             vmem((S, PAD, C // S), F32), vmem((S - 1, PAD, C // S), F32),
             vmem((dims, C // S), F32), vmem((S - 1, dims, C // S), F32),
             vmem((G, 2, PAD, LANES), F32), vmem((G, PAD, LANES), F32), vmem((G, PAD, LANES), F32),
             vmem((G - 1, PAD, LANES), F32),
-            dma((G - 1,)), dma((G - 1,)), dma, dma, dma((S - 1,)), dma((S - 1,)),
-            dma((G - 1,)), dma((G - 1,)), dma, dma, dma((S - 1,)), dma((S - 1,)),
+            dma((G - 1,)), dma((G - 1,)), dma((2,)), dma((2,)), dma((S - 1,)), dma((S - 1,)),
+            dma((G - 1,)), dma((G - 1,)), dma((2,)), dma((2,)), dma((S - 1,)), dma((S - 1,)),
             dma((S - 1,)), dma((S - 1,)), dma((S - 1,)), dma((S - 1,)),
             dma((G,)), dma((G,)), dma((G - 1,)), dma((G - 1,)),
         ],

time: 84.4 us -> 61.2 us (0.73)
  Pallas kernels: 80.5 us -> 57.2 us
    pallas_call x1, Pallas kernels: 80.5 us -> 57.2 us  [shards(): pl.pallas_call(functools.partial(kernel, S, T), out_shape=(jax.ShapeDtype...]
where the time goes in v1:
time: 61.2 us; the launch traced here: 60.9 us
  Pallas kernels  57.2 us (93%)
  local copies, waits for them, and re-layouts  3.05 us (5%)
  between operations  0.64 us (1%)
    pallas_call x1, Pallas kernels, shards(): pl.pallas_call(functools.partial(kernel, S, T), out_shape=(jax.ShapeDtype...  57.2 us
    unnamed x2, local copies, waits for them, and re-layouts  3.05 us

profile of v1, /device:TPU:1, one launch (start us, length us, event | category | flops | bytes accessed | tf_op | source)
XLA Modules:
  0.0 60.9 jit_solution(15058726310009026068)
XLA Ops:
  0.6 57.2 %shard_map.68 = (f32[64,128]{1,0:T(8,128)}, f32[64,1024]{1,0:T(8,128)}) custom-call(f32[64,4096]{1,0:T(8,128)} %x_ref.1, f32[64,1024]{1,0:T(8,128)} %y_ref.1, s32[1,4096]{1,0:T(1,128)} %bitcast.2, s32[1,1024]{1,0:T(1,128)} %bitcast.3, s32[64,64]{1,0:T(8,128)} %mask_ref.1), custom_call_target="tpu_custom_call" | custom-call | tf_op jit(solution)/shard_map/pallas_call | solution.py:413
  57.9 1.4 %copy.9 = f32[64,128]{1,0:T(8,128)} copy(f32[64,128]{1,0:T(8,128)} %get-tuple-element.4) | data formatting | bytes 65536
  59.3 1.7 %copy.10 = f32[64,1024]{1,0:T(8,128)} copy(f32[64,1024]{1,0:T(8,128)} %get-tuple-element.5) | data formatting | bytes 524288

commit v2 on v1

--- a/solution.py
+++ b/solution.py
@@ -19,14 +19,6 @@
 PAD = 72
 
 
-def in_three(value):
-    first = value.astype(BF16)
-    rest = value - first.astype(F32)
-    second = rest.astype(BF16)
-    third = (rest - second.astype(F32)).astype(BF16)
-    return first, second, third
-
-
 def in_two(value):
     first = value.astype(BF16)
     return first, (value - first.astype(F32)).astype(BF16)
@@ -45,8 +37,8 @@
     return pl.ds(pl.multiple_of(index * size, size), size)
 
 
-def kernel(S, T, x_ref, y_ref, sl_ref, tl_ref, mask_ref, so_ref, to_ref,
-           xa, ya, zr, ehi, elo, frow, mp, mb, sp, sb, xw, yw,
+def kernel(S, T, x_hbm, y_ref, sl_ref, tl_ref, mask_ref, so_ref, to_ref,
+           x_ref, nbuf, fetched, xa, ya, zr, ehi, elo, frow, mp, mb, sp, sb, xw, yw,
            lbuf, lrec, lpair, lown, lprec, mbuf, gbuf, grec,
            rbuf, rrec, rpair, rown, rprec, cbuf, crec,
            wbuf, wrec, tbuf, trec, sbuf, prec, pbuf, srec,
@@ -65,8 +57,19 @@
     chip = me_t // 2
     partner = me_t + 1 - 2 * core
 
+    GZ = min(4, G)
+    GX = G // GZ
+    offsets = sorted(
+        ((dx, dz) for dx in range(GX) for dz in range(GZ)),
+        key=lambda d: min(d[0], GX - d[0]) + min(d[1], GZ - d[1]))
+    offsets = offsets[:1] + offsets[:0:-1]
+
+    def chip_at(o):
+        dx, dz = offsets[o]
+        return lax.rem(chip // GZ + dx, GX) * GZ + lax.rem(lax.rem(chip, GZ) + dz, GZ)
+
     def mate(o):
-        return (me_s, lax.rem(me_t + 2 * o, T))
+        return (me_s, 2 * chip_at(o) + core)
 
     def above(o):
         return (lax.rem(me_s + o, S), me_t)
@@ -109,37 +112,47 @@
     def natural(slot):
         return slot + core - 2 * slot * core
 
+    def source_place(c):
+        place = natural(c // (half // XC)) * half + lax.rem(c, half // XC) * XC
+        return pl.ds(pl.multiple_of(place, XC), XC)
+
+    def fetch(c):
+        place = source_place(c)
+        return pltpu.make_async_copy(x_hbm.at[:, place], x_ref.at[:, place], fetched.at[c])
+
+    for c in range(R // XC):
+        fetch(c).start()
+
     def prepare_source(c, _):
         at = span(c, XC)
-        place = natural(c // (half // XC)) * half + lax.rem(c, half // XC) * XC
-        place = pl.ds(pl.multiple_of(place, XC), XC)
+        place = source_place(c)
+        fetch(c).wait()
         x = x_ref[:, place]
-        x1, x2, x3 = in_three(x)
-        for k, part in enumerate((x1, x2, x1, x2, x3, x1)):
+        x1, x2 = in_two(x)
+        for k, part in enumerate((x1, x2, x1)):
             xa[k * dims:(k + 1) * dims, at] = part
         ids = lax.broadcasted_iota(jnp.int32, (dims, XC), 0)
-        xa[6 * dims:7 * dims, at] = jnp.where(ids == sl_ref[:, place], 1.0, 0.0).astype(BF16)
-        n1, n2, n3 = (p.astype(F32) for p in in_three(-scale * jnp.sum(x * x, 0, keepdims=True)))
-        norm = jnp.where(ids == 3, n1, jnp.where(ids == 4, n2, jnp.where(ids == 5, n3, 0.0)))
-        xa[7 * dims:8 * dims, at] = jnp.where(ids < 3, 1.0, norm).astype(BF16)
+        xa[3 * dims:, at] = jnp.where(ids == sl_ref[:, place], 1.0, 0.0).astype(BF16)
+        norm = -scale * jnp.sum(x * x, 0, keepdims=True)
+        for k in range(XC // LANES):
+            nbuf[pl.ds(c * (XC // LANES) + k, 1), :] = norm[:, chunks(k)]
         return 0
 
-    lax.fori_loop(0, R // XC, prepare_source, 0)
-
     y = y_ref[...]
-    y1, y2, y3 = (p.astype(F32) for p in in_three(2.0 * scale * y))
+    y1, y2 = (p.astype(F32) for p in in_two(2.0 * scale * y))
     ids = lax.broadcasted_iota(jnp.int32, (dims, C), 0)
     onehot = jnp.where(ids == tl_ref[...], 1.0, 0.0).astype(BF16)
     allowed = jnp.dot(mask_ref[...].astype(F32).astype(BF16), onehot, preferred_element_type=F32)
     penalty = jnp.where(allowed > 0.5, 0.0, BARRED)
-    n1, n2, n3 = (p.astype(F32) for p in in_three(-scale * jnp.sum(y * y, 0, keepdims=True)))
-    norm = jnp.where(ids == 0, n1, jnp.where(ids == 1, n2, jnp.where(ids == 2, n3, 0.0)))
-    norm = jnp.where((ids >= 3) & (ids < 6), 1.0, norm)
-    for k, (a, b) in enumerate(((y1, y1), (y2, y2), (y1, y3), (penalty, norm))):
+    for k, (a, b) in enumerate(((y1, y1), (y2, penalty))):
         ya[:, k * LANES:(k + 1) * LANES] = jnp.concatenate([a, b], 0).T.astype(BF16)
+    norm = -scale * jnp.sum(y * y, 0, keepdims=True)
+    for b in range(CB):
+        mb[b * LANES:(b + 1) * LANES, :] = turned(norm[:, chunks(b)])
+    lax.fori_loop(0, R // XC, prepare_source, 0)
 
     block = 2 * LANES
-    sub = 8 * GROUP
+    sub = 16 * GROUP
 
     def first_rows(slot):
         behind = None
@@ -148,17 +161,22 @@
             if u < half // block:
                 at = slice(slot * half + u * block, slot * half + (u + 1) * block)
                 z = jnp.dot(ya[...], xa[:, at], preferred_element_type=F32)
-                zr[:, at] = z
-                tops = functools.reduce(
-                    jnp.maximum, [z[k * sub:(k + 1) * sub] for k in range(C // sub)])
-                ahead = at, jnp.max(tops, 0, keepdims=True)
+                ahead = []
+                for k in range(2):
+                    tops = None
+                    for i in range(C // sub):
+                        rows = slice(i * sub, (i + 1) * sub)
+                        part = z[rows, chunks(k)] + mb[rows, :]
+                        zr[slot * half_rows + 2 * u + k, rows, :] = part
+                        tops = part if tops is None else jnp.maximum(tops, part)
+                    ahead.append(jnp.max(tops, 0, keepdims=True))
             if behind is not None:
-                at, top = behind
-                total = sum(
-                    jnp.exp2(zr[k * sub:(k + 1) * sub, at] - top) for k in range(C // sub))
-                lse = top + jnp.log2(jnp.sum(total, 0, keepdims=True))
                 for k in range(2):
-                    lbuf[slot, 2 * (u - 1) + k:2 * (u - 1) + k + 1, :] = lse[:, chunks(k)]
+                    row, top = 2 * (u - 1) + k, behind[k]
+                    total = sum(
+                        jnp.exp2(zr[slot * half_rows + row, i * sub:(i + 1) * sub, :] - top)
+                        for i in range(C // sub))
+                    lbuf[slot, row:row + 1, :] = top + jnp.log2(jnp.sum(total, 0, keepdims=True))
             behind = ahead
 
     first_rows(1)
@@ -171,7 +189,8 @@
     copies = to_mates(lpair, lrec, lsend, lrecv)
     begin(copies)
     finish(copies)
-    lown[...] = -math.log2(R * S) - lse_of([lpair[...]] + [lrec[o] for o in range(G - 1)])
+    lown[...] = -math.log2(R * S) - (
+        lse_of([lpair[...]] + [lrec[o] for o in range(G - 1)]) + nbuf[0:half_rows, :])
     late = remote(lown, lprec.at[1], psend.at[1], precv.at[1], pair)
     late.start()
 
@@ -194,7 +213,7 @@
             acc = [[None, None] for _ in range(WIDE)]
             for q in range(half_rows):
                 row = frow[:, lanes_of(slot, q)]
-                for g, z in enumerate(parts_of(zr[at, lanes_of(slot, q)])):
+                for g, z in enumerate(parts_of(zr[slot * half_rows + q, at, :])):
                     value = step(z, row)
                     old = acc[g][q % 2]
                     acc[g][q % 2] = value if old is None else combine(old, value)
@@ -204,10 +223,10 @@
 
         lax.fori_loop(0, C // (WIDE * GROUP), body, 0)
 
-    spread(0, lown[...])
+    spread(0, lown[...] + nbuf[0:half_rows, :])
     by_rows(0, jnp.add, jnp.maximum, mp, False)
     late.wait()
-    spread(1, lprec[1])
+    spread(1, lprec[1] + nbuf[half_rows:, :])
     by_rows(1, jnp.add, jnp.maximum, mp, True)
 
     for b in range(CB):
@@ -217,18 +236,18 @@
         mb[rows, :] = turned(top)
 
     def weigh(j, _):
-        at = span(j, 2 * GROUP)
+        at = span(j, WIDE * GROUP)
         peak = mb[at, :]
         acc = [None, None]
         for q in range(RB):
-            row = jnp.concatenate([frow[:, chunks(q)]] * 2, 0)
-            e = jnp.exp2(zr[at, chunks(q)] + row - peak)
-            zr[at, chunks(q)] = e
+            row = jnp.concatenate([frow[:, chunks(q)]] * WIDE, 0)
+            e = jnp.exp2(zr[q, at, :] + row - peak)
+            zr[q, at, :] = e
             acc[q % 2] = e if acc[q % 2] is None else acc[q % 2] + e
         sp[at, :] = acc[0] + acc[1]
         return 0
 
-    lax.fori_loop(0, C // (2 * GROUP), weigh, 0)
+    lax.fori_loop(0, C // (WIDE * GROUP), weigh, 0)
     for b in range(CB):
         rows = slice(b * LANES, (b + 1) * LANES)
         total = jnp.sum(sp[rows, :].T, 0, keepdims=True)
@@ -238,14 +257,16 @@
     begin(copies)
 
     def halve(j, _):
-        at = span(j, 2 * GROUP)
-        ehi[at, :], elo[at, :] = in_two(zr[at, :])
+        at = span(j, 4 * GROUP)
+        for q in range(RB):
+            ehi[q, at, :], elo[q, at, :] = in_two(zr[q, at, :])
         return 0
 
-    lax.fori_loop(0, C // (2 * GROUP), halve, 0)
+    lax.fori_loop(0, C // (4 * GROUP), halve, 0)
     finish(copies)
     lse = lse_of([gbuf[...]] + [grec[o] for o in range(S - 1)])
     sig = jnp.exp2(mbuf[...] - lse)
+    mbuf[...] = sig
     for b in range(CB):
         sb[b * LANES:(b + 1) * LANES, :] = turned(sig[b:b + 1, :])
 
@@ -256,7 +277,7 @@
             acc = list(acc)
             weights = parts_of(sb[at, :])
             for q in range(half_rows):
-                terms = [z * w for z, w in zip(parts_of(zr[at, lanes_of(slot, q)]), weights)]
+                terms = [z * w for z, w in zip(parts_of(zr[slot * half_rows + q, at, :]), weights)]
                 acc[q] = acc[q] + ((terms[0] + terms[1]) + (terms[2] + terms[3]))
             return tuple(acc)
 
@@ -311,25 +332,31 @@
 
     across = (((1,), (1,)), ((), ()))
 
-    for k in range(S):
-        at = slice(k * QW, (k + 1) * QW)
-        value, mass = folded(
-            lax.dot_general(xw[...], ehi[at, :], across, preferred_element_type=F32)
-            + lax.dot_general(xw[...], elo[at, :], across, preferred_element_type=F32))
-        for b in range(QW // LANES):
-            row = sig[k * (QW // LANES) + b:k * (QW // LANES) + b + 1, :]
-            wbuf[k, 0:dims, chunks(b)] = value[:, chunks(b)] * row
-            wbuf[k, dims:PAD, chunks(b)] = jnp.broadcast_to(
-                mass[:, chunks(b)] * row, (PAD - dims, LANES))
-    wcopies = [
-        remote(wbuf.at[lax.rem(me_s + o, S)], wrec.at[o - 1], wsend.at[o - 1], wrecv.at[o - 1],
-               above(o)) for o in range(1, S)]
-    begin(wcopies)
-    finish(copies)
-    factor = sig / (cbuf[...] + sum(crec[o] for o in range(S - 1)))
-    for b in range(CB):
-        row = factor[b:b + 1, :]
-        with_mass(yw, chunks(b), y_ref[:, chunks(b)] * row, row)
+    def sent_target(o):
+        return remote(wbuf.at[o], wrec.at[o - 1], wsend.at[o - 1], wrecv.at[o - 1], above(o))
+
+    def target_sums(which):
+        owners = [lax.rem(me_s + o, S) for o in which]
+        outs = [None] * len(which)
+        depth = min(8, RB)
+        for k in range(0, RB, depth):
+            left = xw[:, k * LANES:(k + depth) * LANES]
+            for ref in (ehi, elo):
+                for i, owner in enumerate(owners):
+                    at = span(owner, QW)
+                    right = jnp.concatenate([ref[q, at, :] for q in range(k, k + depth)], 1)
+                    part = lax.dot_general(left, right, across, preferred_element_type=F32)
+                    outs[i] = part if outs[i] is None else outs[i] + part
+        for o, owner, out in zip(which, owners, outs):
+            value, mass = folded(out)
+            for b in range(QW // LANES):
+                row = mbuf[pl.ds(owner * (QW // LANES) + b, 1), :]
+                wbuf[o, 0:dims, chunks(b)] = value[:, chunks(b)] * row
+                wbuf[o, dims:PAD, chunks(b)] = jnp.broadcast_to(
+                    mass[:, chunks(b)] * row, (PAD - dims, LANES))
+        for o in which:
+            if o:
+                sent_target(o).start()
 
     def to_partner(o):
         return remote(sbuf.at[o, 1 - core], prec.at[o], bsend.at[o], brecv.at[o], pair)
@@ -338,58 +365,61 @@
         return remote(pbuf.at[o], srec.at[o - 1], ssend.at[o - 1], srecv.at[o - 1], mate(o))
 
     def source_sums(o):
-        owner = lax.rem(chip + o, G)
-        place = natural(owner // (G // 2)) * half + lax.rem(owner, G // 2) * (2 * LANES)
-        at = pl.ds(pl.multiple_of(place, 2 * LANES), 2 * LANES)
+        owner = chip_at(o)
+        place = natural(owner // (G // 2)) * half_rows + lax.rem(owner, G // 2) * 2
+
+        def wide(ref):
+            return jnp.concatenate([ref[place], ref[place + 1]], 1)
+
         value, mass = folded(
-            jnp.dot(yw[...], ehi[:, at], preferred_element_type=F32)
-            + jnp.dot(yw[...], elo[:, at], preferred_element_type=F32))
+            jnp.dot(yw[...], wide(ehi), preferred_element_type=F32)
+            + jnp.dot(yw[...], wide(elo), preferred_element_type=F32))
         for k in range(2):
             sbuf[o, k, 0:dims, :] = value[:, chunks(k)]
             sbuf[o, k, dims:PAD, :] = jnp.broadcast_to(mass[:, chunks(k)], (PAD - dims, LANES))
 
-    def pass_on(o):
-        to_partner(o).wait_recv()
-        pbuf[o] = sbuf[o, core] + prec[o]
-
-    V = min(4, G)
-
-    def compute(g):
-        for v in range(V):
-            source_sums(lax.rem(g * V + v + 1, G))
-        for v in range(V):
-            to_partner(lax.rem(g * V + v + 1, G)).start()
-
-    def relay(g):
-        for v in range(V):
-            pass_on(g * V + v + 1)
-            to_owner(g * V + v + 1).start()
-
-    compute(0)
-
-    def source_step(g, _):
-        compute(g + 1)
-        relay(g)
-        return 0
-
-    lax.fori_loop(0, G // V - 1, source_step, 0)
-    for v in range(G - V + 1, G):
-        pass_on(v)
-        to_owner(v).start()
-    pass_on(0)
-
-    finish(wcopies)
-    total = wbuf[me_s] + sum(wrec[o] for o in range(S - 1))
-    tbuf[...] = total[0:dims] / total[dims:dims + 1]
-    tcopies = to_column(tbuf, trec, tsend, trecv)
-    begin(tcopies)
-    to_ref[:, span(me_s, QW)] = tbuf[...]
-
-    def settle(o, acc):
+    V = max(1, G // 4)
+    order = [o % G for o in range(1, G + 1)]
+    sets = [order[i:i + V] for i in range(0, G, V)]
+
+    def compute(which):
+        for o in which:
+            source_sums(o)
+        for o in which:
+            to_partner(o).start()
+
+    def relay(which):
+        for o in which:
+            to_partner(o).wait_recv()
+            pbuf[o] = sbuf[o, core] + prec[o]
+            if o:
+                to_owner(o).start()
+
+    turns = list(range(1, S)) + [0]
+    target_sums(turns[:2])
+    finish(copies)
+    factor = sig / (cbuf[...] + sum(crec[o] for o in range(S - 1)))
+    for b in range(CB):
+        row = factor[b:b + 1, :]
+        with_mass(yw, chunks(b), y_ref[:, chunks(b)] * row, row)
+    rest = turns[2:]
+    for k, which in enumerate(sets):
+        compute(which)
+        if k == 0 and rest:
+            target_sums(rest)
+        if k == 2 or k == len(sets) - 1 < 2:
+            finish([sent_target(o) for o in range(1, S)])
+            total = wbuf[0] + sum(wrec[o] for o in range(S - 1))
+            tbuf[...] = total[0:dims] / total[dims:dims + 1]
+            tcopies = to_column(tbuf, trec, tsend, trecv)
+            begin(tcopies)
+            to_ref[:, span(me_s, QW)] = tbuf[...]
+        relay(which)
+
+    total = pbuf[0]
+    for o in range(1, G):
         to_owner(o).wait()
-        return acc + srec[o - 1]
-
-    total = lax.fori_loop(1, G, settle, pbuf[0])
+        total = total + srec[o - 1]
     so_ref[...] = total[0:dims] / total[dims:dims + 1]
 
     def sent(o, _):
@@ -400,6 +430,11 @@
     finish(tcopies)
     for o in range(1, S):
         to_ref[:, span(lax.rem(me_s + S - o, S), QW)] = trec[o - 1]
+
+
+def delivered(s_ref, t_ref, so_ref, to_ref):
+    so_ref[...] = s_ref[...]
+    to_ref[...] = t_ref[...]
 
 
 def shards(S, T, source_pca, target_pca, source_labels, target_labels, block_mask):
@@ -410,14 +445,15 @@
     vmem = pltpu.VMEM
     dma = pltpu.SemaphoreType.DMA
     whole = pl.BlockSpec(memory_space=pltpu.VMEM)
-    return pl.pallas_call(
+    raw = pl.pallas_call(
         functools.partial(kernel, S, T),
         out_shape=(jax.ShapeDtypeStruct((dims, R // T), F32), jax.ShapeDtypeStruct((dims, C), F32)),
-        in_specs=[whole] * 5,
+        in_specs=[pl.BlockSpec(memory_space=pl.ANY)] + [whole] * 4,
         out_specs=(whole, whole),
         scratch_shapes=[
-            vmem((8 * dims, R), BF16), vmem((C, 8 * dims), BF16), vmem((C, R), F32),
-            vmem((C, R), BF16), vmem((C, R), BF16), vmem((GROUP, R), F32),
+            vmem((dims, R), F32), vmem((RB, LANES), F32), dma((R // min(512, R // 2),)),
+            vmem((4 * dims, R), BF16), vmem((C, 4 * dims), BF16), vmem((RB, C, LANES), F32),
+            vmem((RB, C, LANES), BF16), vmem((RB, C, LANES), BF16), vmem((GROUP, R), F32),
             vmem((C, LANES), F32), vmem((C, LANES), F32), vmem((C, LANES), F32),
             vmem((C, LANES), F32),
             vmem((2 * dims + 2 * GROUP, R), BF16), vmem((2 * dims + 2 * GROUP, C), BF16),
@@ -439,6 +475,12 @@
         compiler_params=pltpu.CompilerParams(
             collective_id=0, has_side_effects=True, vmem_limit_bytes=60 * 2**20),
     )(source_pca, target_pca, source_labels.reshape(1, R), target_labels.reshape(1, C), block_mask)
+    return pl.pallas_call(
+        delivered,
+        out_shape=tuple(jax.ShapeDtypeStruct(r.shape, F32) for r in raw),
+        in_specs=[whole] * 2,
+        out_specs=(whole, whole),
+    )(*raw)
 
 
 def solution(mesh):

time: 61.2 us -> 56.9 us (0.930)
  local copies, waits for them, and re-layouts: 3.05 us -> 0 us
  Pallas kernels: 57.2 us -> 56.1 us
    unnamed x2 -> x0, local copies, waits for them, and re-layouts: 3.05 us -> none
    pallas_call x1, Pallas kernels: 57.2 us -> 54.4 us  [shards(): pl.pallas_call(functools.partial(kernel, S, T), out_shape=(jax.ShapeDtype...]
    pallas_call x0 -> x1, Pallas kernels: none -> 1.69 us  [shards(): pl.pallas_call(delivered, out_shape=tuple((jax.ShapeDtypeStruct(r.shape,...]
where the time goes in v2:
time: 56.9 us; the launch traced here: 56.7 us
  Pallas kernels  56.1 us (99%)
  between operations  0.64 us (1%)
    pallas_call x1, Pallas kernels, shards(): pl.pallas_call(functools.partial(kernel, S, T), out_shape=(jax.ShapeDtype...  54.4 us
    pallas_call x1, Pallas kernels, shards(): pl.pallas_call(delivered, out_shape=tuple((jax.ShapeDtypeStruct(r.shape,...  1.69 us

profile of v2, /device:TPU:1, one launch (start us, length us, event | category | flops | bytes accessed | tf_op | source)
XLA Modules:
  0.0 56.7 jit_solution(1773302009064140269)
XLA Ops:
  0.6 54.4 %shard_map.68 = (f32[64,128]{1,0:T(8,128)}, f32[64,1024]{1,0:T(8,128)}) custom-call(f32[64,4096]{1,0:T(8,128)} %x_hbm.1, f32[64,1024]{1,0:T(8,128)} %y_ref.1, s32[1,4096]{1,0:T(1,128)} %bitcast.2, s32[1,1024]{1,0:T(1,128)} %bitcast.3, s32[64,64]{1,0:T(8,128)} %mask_ref.1), custom_call_target="tpu_custom_call" | custom-call | tf_op jit(solution)/shard_map/pallas_call | solution.py:448
  55.0 1.7 %shard_map.69 = (f32[64,128]{1,0:T(8,128)}, f32[64,1024]{1,0:T(8,128)}) custom-call(f32[64,128]{1,0:T(8,128)} %get-tuple-element.4.s_ref, f32[64,1024]{1,0:T(8,128)} %get-tuple-element.5.t_ref), custom_call_target="tpu_custom_call" | custom-call | tf_op jit(solution)/shard_map/pallas_call | solution.py:478

commit v3 on v2

--- a/solution.py
+++ b/solution.py
@@ -86,20 +86,17 @@
             device_id=device, device_id_type=MESH)
 
     def to_mates(src, dst, send, recv):
-        return [remote(src, dst.at[o - 1], send.at[o - 1], recv.at[o - 1], mate(o))
-                for o in range(1, G)]
+        return [remote(src, dst.at[o - 1], send, recv, mate(o)) for o in range(1, G)]
 
     def to_column(src, dst, send, recv):
-        return [remote(src, dst.at[o - 1], send.at[o - 1], recv.at[o - 1], above(o))
-                for o in range(1, S)]
+        return [remote(src, dst.at[o - 1], send, recv, above(o)) for o in range(1, S)]
+
+    def all_of(dst, send, recv):
+        return remote(dst, dst, send, recv, pair)
 
     def begin(copies):
         for copy in copies:
             copy.start()
-
-    def finish(copies):
-        for copy in copies:
-            copy.wait()
 
     def chunks(q):
         return slice(q * LANES, (q + 1) * LANES)
@@ -186,9 +183,8 @@
     first_rows(0)
     early.wait()
     lpair[...] = lse_of([lbuf[0], lprec[0]])
-    copies = to_mates(lpair, lrec, lsend, lrecv)
-    begin(copies)
-    finish(copies)
+    begin(to_mates(lpair, lrec, lsend, lrecv))
+    all_of(lrec, lsend, lrecv).wait()
     lown[...] = -math.log2(R * S) - (
         lse_of([lpair[...]] + [lrec[o] for o in range(G - 1)]) + nbuf[0:half_rows, :])
     late = remote(lown, lprec.at[1], psend.at[1], precv.at[1], pair)
@@ -253,8 +249,7 @@
         total = jnp.sum(sp[rows, :].T, 0, keepdims=True)
         gbuf[b:b + 1, :] = mbuf[b:b + 1, :] + jnp.log2(total)
 
-    copies = to_column(gbuf, grec, gsend, grecv)
-    begin(copies)
+    begin(to_column(gbuf, grec, gsend, grecv))
 
     def halve(j, _):
         at = span(j, 4 * GROUP)
@@ -263,7 +258,7 @@
         return 0
 
     lax.fori_loop(0, C // (4 * GROUP), halve, 0)
-    finish(copies)
+    all_of(grec, gsend, grecv).wait()
     lse = lse_of([gbuf[...]] + [grec[o] for o in range(S - 1)])
     sig = jnp.exp2(mbuf[...] - lse)
     mbuf[...] = sig
@@ -292,9 +287,8 @@
     row_mass(0)
     early.wait()
     rpair[...] = rbuf[0] + rprec[0]
-    copies = to_mates(rpair, rrec, rsend, rrecv)
-    begin(copies)
-    finish(copies)
+    begin(to_mates(rpair, rrec, rsend, rrecv))
+    all_of(rrec, rsend, rrecv).wait()
     rown[...] = (C * T / (R * S)) / (rpair[...] + sum(rrec[o] for o in range(G - 1)))
     late = remote(rown, rprec.at[1], qsend.at[1], qrecv.at[1], pair)
     late.start()
@@ -306,8 +300,7 @@
     for b in range(CB):
         rows = slice(b * LANES, (b + 1) * LANES)
         cbuf[b:b + 1, :] = sig[b:b + 1, :] * jnp.sum(sp[rows, :].T, 0, keepdims=True)
-    copies = to_column(cbuf, crec, csend, crecv)
-    begin(copies)
+    begin(to_column(cbuf, crec, csend, crecv))
 
     tail = lax.broadcasted_iota(jnp.int32, (2 * GROUP, LANES), 0)
 
@@ -333,36 +326,45 @@
     across = (((1,), (1,)), ((), ()))
 
     def sent_target(o):
-        return remote(wbuf.at[o], wrec.at[o - 1], wsend.at[o - 1], wrecv.at[o - 1], above(o))
-
-    def target_sums(which):
-        owners = [lax.rem(me_s + o, S) for o in which]
-        outs = [None] * len(which)
+        return remote(wbuf.at[o], wrec.at[o - 1], wsend, wrecv, above(o))
+
+    def target_sums(*which):
+        width = QW if len(which) > 1 else LANES
+        pieces = [(o, p) for o in which for p in range(0, QW, width)]
+        owner = [lax.rem(me_s + o, S) for o in range(S)]
+        outs = [None] * len(pieces)
         depth = min(8, RB)
         for k in range(0, RB, depth):
             left = xw[:, k * LANES:(k + depth) * LANES]
             for ref in (ehi, elo):
-                for i, owner in enumerate(owners):
-                    at = span(owner, QW)
+                for i, (o, p) in enumerate(pieces):
+                    at = pl.ds(pl.multiple_of(owner[o] * QW + p, width), width)
                     right = jnp.concatenate([ref[q, at, :] for q in range(k, k + depth)], 1)
                     part = lax.dot_general(left, right, across, preferred_element_type=F32)
                     outs[i] = part if outs[i] is None else outs[i] + part
-        for o, owner, out in zip(which, owners, outs):
+        for (o, p), out in zip(pieces, outs):
             value, mass = folded(out)
-            for b in range(QW // LANES):
-                row = mbuf[pl.ds(owner * (QW // LANES) + b, 1), :]
-                wbuf[o, 0:dims, chunks(b)] = value[:, chunks(b)] * row
-                wbuf[o, dims:PAD, chunks(b)] = jnp.broadcast_to(
+            for b in range(width // LANES):
+                at = slice(p + b * LANES, p + (b + 1) * LANES)
+                row = mbuf[pl.ds(owner[o] * (QW // LANES) + p // LANES + b, 1), :]
+                wbuf[o, 0:dims, at] = value[:, chunks(b)] * row
+                wbuf[o, dims:PAD, at] = jnp.broadcast_to(
                     mass[:, chunks(b)] * row, (PAD - dims, LANES))
         for o in which:
             if o:
                 sent_target(o).start()
 
-    def to_partner(o):
-        return remote(sbuf.at[o, 1 - core], prec.at[o], bsend.at[o], brecv.at[o], pair)
+    V = max(1, G // 4)
+    order = [o % G for o in range(1, G + 1)]
+    sets = [order[i:i + V] for i in range(0, G, V)]
+
+    def to_partner(k):
+        at = pl.ds(k * V, V)
+        return remote(sbuf.at[1 - core, at], prec.at[at], bsend.at[k], brecv.at[k], pair)
 
     def to_owner(o):
-        return remote(pbuf.at[o], srec.at[o - 1], ssend.at[o - 1], srecv.at[o - 1], mate(o))
+        rows = pl.ds(0, dims + 1)
+        return remote(pbuf.at[o, rows], srec.at[o - 1, rows], ssend, srecv, mate(o))
 
     def source_sums(o):
         owner = chip_at(o)
@@ -375,66 +377,67 @@
             jnp.dot(yw[...], wide(ehi), preferred_element_type=F32)
             + jnp.dot(yw[...], wide(elo), preferred_element_type=F32))
         for k in range(2):
-            sbuf[o, k, 0:dims, :] = value[:, chunks(k)]
-            sbuf[o, k, dims:PAD, :] = jnp.broadcast_to(mass[:, chunks(k)], (PAD - dims, LANES))
-
-    V = max(1, G // 4)
-    order = [o % G for o in range(1, G + 1)]
-    sets = [order[i:i + V] for i in range(0, G, V)]
-
-    def compute(which):
-        for o in which:
+            sbuf[k, (o - 1) % G, 0:dims, :] = value[:, chunks(k)]
+            sbuf[k, (o - 1) % G, dims:PAD, :] = jnp.broadcast_to(
+                mass[:, chunks(k)], (PAD - dims, LANES))
+
+    def compute(k):
+        for o in sets[k]:
             source_sums(o)
-        for o in which:
-            to_partner(o).start()
-
-    def relay(which):
-        for o in which:
-            to_partner(o).wait_recv()
-            pbuf[o] = sbuf[o, core] + prec[o]
+        to_partner(k).start()
+
+    def relay(k):
+        to_partner(k).wait_recv()
+        for o in sets[k]:
+            pbuf[o] = sbuf[core, (o - 1) % G] + prec[(o - 1) % G]
+        for o in sets[k]:
             if o:
                 to_owner(o).start()
 
-    turns = list(range(1, S)) + [0]
-    target_sums(turns[:2])
-    finish(copies)
+    for o in range(1, S, 2):
+        target_sums(*range(o, min(o + 2, S)))
+    all_of(crec, csend, crecv).wait()
     factor = sig / (cbuf[...] + sum(crec[o] for o in range(S - 1)))
     for b in range(CB):
         row = factor[b:b + 1, :]
         with_mass(yw, chunks(b), y_ref[:, chunks(b)] * row, row)
-    rest = turns[2:]
-    for k, which in enumerate(sets):
-        compute(which)
-        if k == 0 and rest:
-            target_sums(rest)
-        if k == 2 or k == len(sets) - 1 < 2:
-            finish([sent_target(o) for o in range(1, S)])
-            total = wbuf[0] + sum(wrec[o] for o in range(S - 1))
-            tbuf[...] = total[0:dims] / total[dims:dims + 1]
-            tcopies = to_column(tbuf, trec, tsend, trecv)
-            begin(tcopies)
-            to_ref[:, span(me_s, QW)] = tbuf[...]
-        relay(which)
-
-    total = pbuf[0]
-    for o in range(1, G):
-        to_owner(o).wait()
-        total = total + srec[o - 1]
-    so_ref[...] = total[0:dims] / total[dims:dims + 1]
-
-    def sent(o, _):
-        to_partner(o).wait_send()
-        return 0
-
-    lax.fori_loop(0, G, sent, 0)
-    finish(tcopies)
+    compute(0)
+    compute(1)
+    relay(0)
+    target_sums(0)
+    relay(1)
+    if len(sets) > 2:
+        compute(2)
+    all_of(wrec, wsend, wrecv).wait()
+    total = wbuf[0] + sum(wrec[o] for o in range(S - 1))
+    tbuf[...] = total[0:dims] / total[dims:dims + 1]
+    begin(to_column(tbuf, trec, tsend, trecv))
+    to_ref[:, span(me_s, QW)] = tbuf[...]
+    for k in range(2, len(sets)):
+        relay(k)
+        if k + 1 < len(sets):
+            compute(k + 1)
+
+    arrived = srec.at[:, pl.ds(0, dims + 1)]
+    remote(arrived, arrived, ssend, srecv, pair).wait()
+    total = pbuf[0, 0:dims] + sum(srec[o, 0:dims] for o in range(G - 1))
+    mass = pbuf[0, dims:dims + 1] + sum(srec[o, dims:dims + 1] for o in range(G - 1))
+    so_ref[...] = total / mass
+
+    for k in range(len(sets)):
+        to_partner(k).wait_send()
+    all_of(trec, tsend, trecv).wait()
     for o in range(1, S):
         to_ref[:, span(lax.rem(me_s + S - o, S), QW)] = trec[o - 1]
 
 
-def delivered(s_ref, t_ref, so_ref, to_ref):
-    so_ref[...] = s_ref[...]
-    to_ref[...] = t_ref[...]
+def delivered(s_ref, t_ref, so_hbm, to_hbm, sems):
+    copies = [pltpu.make_async_copy(src, dst, sems.at[k])
+              for k, (src, dst) in enumerate(((t_ref, to_hbm), (s_ref, so_hbm)))]
+    for copy in copies:
+        copy.start()
+    for copy in copies:
+        copy.wait()
 
 
 def shards(S, T, source_pca, target_pca, source_labels, target_labels, block_mask):
@@ -442,12 +445,13 @@
     C = target_pca.shape[1]
     G = T // 2
     CB, RB = C // LANES, R // LANES
+    sets = min(4, G)
     vmem = pltpu.VMEM
     dma = pltpu.SemaphoreType.DMA
     whole = pl.BlockSpec(memory_space=pltpu.VMEM)
     raw = pl.pallas_call(
         functools.partial(kernel, S, T),
-        out_shape=(jax.ShapeDtypeStruct((dims, R // T), F32), jax.ShapeDtypeStruct((dims, C), F32)),
+        out_shape=(vmem((dims, R // T), F32), vmem((dims, C), F32)),
         in_specs=[pl.BlockSpec(memory_space=pl.ANY)] + [whole] * 4,
         out_specs=(whole, whole),
         scratch_shapes=[
@@ -465,22 +469,22 @@
             vmem((CB, LANES), F32), vmem((S - 1, CB, LANES), F32),
             vmem((S, PAD, C // S), F32), vmem((S - 1, PAD, C // S), F32),
             vmem((dims, C // S), F32), vmem((S - 1, dims, C // S), F32),
-            vmem((G, 2, PAD, LANES), F32), vmem((G, PAD, LANES), F32), vmem((G, PAD, LANES), F32),
+            vmem((2, G, PAD, LANES), F32), vmem((G, PAD, LANES), F32), vmem((G, PAD, LANES), F32),
             vmem((G - 1, PAD, LANES), F32),
-            dma((G - 1,)), dma((G - 1,)), dma((2,)), dma((2,)), dma((S - 1,)), dma((S - 1,)),
-            dma((G - 1,)), dma((G - 1,)), dma((2,)), dma((2,)), dma((S - 1,)), dma((S - 1,)),
-            dma((S - 1,)), dma((S - 1,)), dma((S - 1,)), dma((S - 1,)),
-            dma((G,)), dma((G,)), dma((G - 1,)), dma((G - 1,)),
+            dma, dma, dma((2,)), dma((2,)), dma, dma,
+            dma, dma, dma((2,)), dma((2,)), dma, dma,
+            dma, dma, dma, dma, dma((sets,)), dma((sets,)), dma, dma,
         ],
         compiler_params=pltpu.CompilerParams(
-            collective_id=0, has_side_effects=True, vmem_limit_bytes=60 * 2**20),
+            collective_id=0, has_side_effects=True, vmem_limit_bytes=56 * 2**20),
     )(source_pca, target_pca, source_labels.reshape(1, R), target_labels.reshape(1, C), block_mask)
     return pl.pallas_call(
         delivered,
         out_shape=tuple(jax.ShapeDtypeStruct(r.shape, F32) for r in raw),
         in_specs=[whole] * 2,
-        out_specs=(whole, whole),
-    )(*raw)
+        out_specs=(pl.BlockSpec(memory_space=pl.ANY),) * 2,
+        scratch_shapes=[dma((2,))],
+    )(*(pltpu.with_memory_space_constraint(r, pltpu.VMEM) for r in raw))
 
 
 def solution(mesh):

time: 56.9 us -> 53.2 us (0.935)
  Pallas kernels: 56.1 us -> 52.3 us
    pallas_call x1, Pallas kernels: 54.4 us -> 51.6 us  [shards(): pl.pallas_call(functools.partial(kernel, S, T), out_shape=(vmem((dims, R...]
    pallas_call x1, Pallas kernels: 1.69 us -> 0.72 us  [shards(): pl.pallas_call(delivered, out_shape=tuple((jax.ShapeDtypeStruct(r.shape,...]
where the time goes in v3:
time: 53.2 us; the launch traced here: 53.1 us
  Pallas kernels  52.3 us (98%)
  between operations  0.8 us (2%)
    pallas_call x1, Pallas kernels, shards(): pl.pallas_call(functools.partial(kernel, S, T), out_shape=(vmem((dims, R...  51.6 us

profile of v3, /device:TPU:1, one launch (start us, length us, event | category | flops | bytes accessed | tf_op | source)
XLA Modules:
  0.0 53.1 jit_solution(6032582617045188399)
XLA Ops:
  0.6 51.6 %shard_map.68 = (f32[64,128]{1,0:T(8,128)S(1)}, f32[64,1024]{1,0:T(8,128)S(1)}) custom-call(f32[64,4096]{1,0:T(8,128)} %x_hbm.1, f32[64,1024]{1,0:T(8,128)} %y_ref.1, s32[1,4096]{1,0:T(1,128)} %bitcast.2, s32[1,1024]{1,0:T(1,128)} %bitcast.3, s32[64,64]{1,0:T(8,128)} %mask_ref.1), custom_call_target="tpu_custom_call" | custom-call | tf_op jit(solution)/shard_map/pallas_call | solution.py:452
  52.2 0.7 %shard_map.69 = (f32[64,128]{1,0:T(8,128)}, f32[64,1024]{1,0:T(8,128)}) custom-call(f32[64,128]{1,0:T(8,128)S(1)} %get-tuple-element.4.s_ref, f32[64,1024]{1,0:T(8,128)S(1)} %get-tuple-element.5.t_ref), custom_call_target="tpu_custom_call" | custom-call | tf_op jit(solution)/shard_map/pallas_call | solution.py:481

commit v4 on v3

--- a/solution.py
+++ b/solution.py
@@ -292,8 +292,26 @@
     rown[...] = (C * T / (R * S)) / (rpair[...] + sum(rrec[o] for o in range(G - 1)))
     late = remote(rown, rprec.at[1], qsend.at[1], qrecv.at[1], pair)
     late.start()
+    tail = lax.broadcasted_iota(jnp.int32, (2 * GROUP, LANES), 0)
+
+    def with_mass(dst, at, value, mass):
+        hi, lo = in_two(value)
+        dst[0:dims, at] = hi
+        dst[dims:2 * dims, at] = lo
+        m1, m2 = (p.astype(F32) for p in in_two(mass))
+        dst[2 * dims:2 * dims + 2 * GROUP, at] = jnp.where(
+            tail == 0, m1, jnp.where(tail == 1, m2, 0.0)).astype(BF16)
+
+    def scale_source(slot):
+        for q in range(slot * half_rows, (slot + 1) * half_rows):
+            row = frow[0:1, chunks(q)]
+            place = natural(slot) * half + (q % half_rows) * LANES
+            place = pl.ds(pl.multiple_of(place, LANES), LANES)
+            with_mass(xw, chunks(q), x_ref[:, place] * row, row)
+
     spread(0, rown[...])
     by_rows(0, jnp.multiply, jnp.add, sp, False)
+    scale_source(0)
     late.wait()
     spread(1, rprec[1])
     by_rows(1, jnp.multiply, jnp.add, sp, True)
@@ -302,21 +320,7 @@
         cbuf[b:b + 1, :] = sig[b:b + 1, :] * jnp.sum(sp[rows, :].T, 0, keepdims=True)
     begin(to_column(cbuf, crec, csend, crecv))
 
-    tail = lax.broadcasted_iota(jnp.int32, (2 * GROUP, LANES), 0)
-
-    def with_mass(dst, at, value, mass):
-        hi, lo = in_two(value)
-        dst[0:dims, at] = hi
-        dst[dims:2 * dims, at] = lo
-        m1, m2 = (p.astype(F32) for p in in_two(mass))
-        dst[2 * dims:2 * dims + 2 * GROUP, at] = jnp.where(
-            tail == 0, m1, jnp.where(tail == 1, m2, 0.0)).astype(BF16)
-
-    for q in range(RB):
-        row = frow[0:1, chunks(q)]
-        place = natural(q // half_rows) * half + (q % half_rows) * LANES
-        place = pl.ds(pl.multiple_of(place, LANES), LANES)
-        with_mass(xw, chunks(q), x_ref[:, place] * row, row)
+    scale_source(1)
 
     def folded(out):
         value = out[0:dims] + out[dims:2 * dims]
@@ -394,8 +398,7 @@
             if o:
                 to_owner(o).start()
 
-    for o in range(1, S, 2):
-        target_sums(*range(o, min(o + 2, S)))
+    target_sums(*range(1, min(3, S)))
     all_of(crec, csend, crecv).wait()
     factor = sig / (cbuf[...] + sum(crec[o] for o in range(S - 1)))
     for b in range(CB):
@@ -404,19 +407,21 @@
     compute(0)
     compute(1)
     relay(0)
+    if S > 3:
+        target_sums(*range(3, S))
+    relay(1)
+    for k in range(2, len(sets)):
+        compute(k)
+    for k in range(2, len(sets) - 1):
+        relay(k)
     target_sums(0)
-    relay(1)
     if len(sets) > 2:
-        compute(2)
+        relay(len(sets) - 1)
     all_of(wrec, wsend, wrecv).wait()
     total = wbuf[0] + sum(wrec[o] for o in range(S - 1))
     tbuf[...] = total[0:dims] / total[dims:dims + 1]
     begin(to_column(tbuf, trec, tsend, trecv))
     to_ref[:, span(me_s, QW)] = tbuf[...]
-    for k in range(2, len(sets)):
-        relay(k)
-        if k + 1 < len(sets):
-            compute(k + 1)
 
     arrived = srec.at[:, pl.ds(0, dims + 1)]
     remote(arrived, arrived, ssend, srecv, pair).wait()

time: 53.2 us -> 52 us (0.977)
  Pallas kernels: 52.3 us -> 51.2 us
    pallas_call x1, Pallas kernels: 51.6 us -> 50.5 us  [shards(): pl.pallas_call(functools.partial(kernel, S, T), out_shape=(vmem((dims, R...]
where the time goes in v4:
time: 52 us; the launch traced here: 51.9 us
  Pallas kernels  51.2 us (98%)
  between operations  0.64 us (1%)
    pallas_call x1, Pallas kernels, shards(): pl.pallas_call(functools.partial(kernel, S, T), out_shape=(vmem((dims, R...  50.5 us

profile of v4, /device:TPU:1, one launch (start us, length us, event | category | flops | bytes accessed | tf_op | source)
XLA Modules:
  0.0 51.9 jit_solution(10872893369729628684)
XLA Ops:
  0.6 50.5 %shard_map.68 = (f32[64,128]{1,0:T(8,128)S(1)}, f32[64,1024]{1,0:T(8,128)S(1)}) custom-call(f32[64,4096]{1,0:T(8,128)} %x_hbm.1, f32[64,1024]{1,0:T(8,128)} %y_ref.1, s32[1,4096]{1,0:T(1,128)} %bitcast.2, s32[1,1024]{1,0:T(1,128)} %bitcast.3, s32[64,64]{1,0:T(8,128)} %mask_ref.1), custom_call_target="tpu_custom_call" | custom-call | tf_op jit(solution)/shard_map/pallas_call | solution.py:457
  51.1 0.7 %shard_map.69 = (f32[64,128]{1,0:T(8,128)}, f32[64,1024]{1,0:T(8,128)}) custom-call(f32[64,128]{1,0:T(8,128)S(1)} %get-tuple-element.4.s_ref, f32[64,1024]{1,0:T(8,128)S(1)} %get-tuple-element.5.t_ref), custom_call_target="tpu_custom_call" | custom-call | tf_op jit(solution)/shard_map/pallas_call | solution.py:486

commit v5 on v4

--- a/solution.py
+++ b/solution.py
@@ -38,7 +38,7 @@
 
 
 def kernel(S, T, x_hbm, y_ref, sl_ref, tl_ref, mask_ref, so_ref, to_ref,
-           x_ref, nbuf, fetched, xa, ya, zr, ehi, elo, frow, mp, mb, sp, sb, xw, yw,
+           x_ref, nbuf, ylow, fetched, xa, ya, zr, ehi, elo, frow, mp, mb, sp, sb, xw, yw,
            lbuf, lrec, lpair, lown, lprec, mbuf, gbuf, grec,
            rbuf, rrec, rpair, rown, rprec, cbuf, crec,
            wbuf, wrec, tbuf, trec, sbuf, prec, pbuf, srec,
@@ -140,40 +140,46 @@
     ids = lax.broadcasted_iota(jnp.int32, (dims, C), 0)
     onehot = jnp.where(ids == tl_ref[...], 1.0, 0.0).astype(BF16)
     allowed = jnp.dot(mask_ref[...].astype(F32).astype(BF16), onehot, preferred_element_type=F32)
-    penalty = jnp.where(allowed > 0.5, 0.0, BARRED)
+    norm = -scale * jnp.sum(y * y, 0, keepdims=True)
+    rounded = norm.astype(BF16).astype(F32)
+    penalty = jnp.where(allowed > 0.5, rounded, BARRED)
     for k, (a, b) in enumerate(((y1, y1), (y2, penalty))):
         ya[:, k * LANES:(k + 1) * LANES] = jnp.concatenate([a, b], 0).T.astype(BF16)
-    norm = -scale * jnp.sum(y * y, 0, keepdims=True)
+    remainder = norm - rounded
     for b in range(CB):
-        mb[b * LANES:(b + 1) * LANES, :] = turned(norm[:, chunks(b)])
+        ylow[b:b + 1, :] = remainder[:, chunks(b)]
+        mb[b * LANES:(b + 1) * LANES, :] = turned(jnp.exp2(remainder[:, chunks(b)]))
     lax.fori_loop(0, R // XC, prepare_source, 0)
 
-    block = 2 * LANES
-    sub = 16 * GROUP
+    block = min(2 * LANES, half)
+    sub = 4 * GROUP
 
     def first_rows(slot):
         behind = None
+        wide = block // LANES
         for u in range(half // block + 1):
             ahead = None
             if u < half // block:
                 at = slice(slot * half + u * block, slot * half + (u + 1) * block)
                 z = jnp.dot(ya[...], xa[:, at], preferred_element_type=F32)
                 ahead = []
-                for k in range(2):
-                    tops = None
-                    for i in range(C // sub):
-                        rows = slice(i * sub, (i + 1) * sub)
-                        part = z[rows, chunks(k)] + mb[rows, :]
-                        zr[slot * half_rows + 2 * u + k, rows, :] = part
-                        tops = part if tops is None else jnp.maximum(tops, part)
+                for k in range(wide):
+                    zr[slot * half_rows + wide * u + k] = z[:, chunks(k)]
+                    tops = functools.reduce(
+                        jnp.maximum, [z[i:i + sub, chunks(k)] for i in range(0, C, sub)])
                     ahead.append(jnp.max(tops, 0, keepdims=True))
             if behind is not None:
-                for k in range(2):
-                    row, top = 2 * (u - 1) + k, behind[k]
-                    total = sum(
-                        jnp.exp2(zr[slot * half_rows + row, i * sub:(i + 1) * sub, :] - top)
-                        for i in range(C // sub))
-                    lbuf[slot, row:row + 1, :] = top + jnp.log2(jnp.sum(total, 0, keepdims=True))
+                totals = [None] * wide
+                for i in range(0, C, sub):
+                    weight = mb[i:i + sub, :]
+                    for k in range(wide):
+                        row = slot * half_rows + wide * (u - 1) + k
+                        e = jnp.exp2(zr[row, i:i + sub, :] - behind[k]) * weight
+                        totals[k] = e if totals[k] is None else totals[k] + e
+                for k in range(wide):
+                    row = wide * (u - 1) + k
+                    lbuf[slot, row:row + 1, :] = behind[k] + jnp.log2(
+                        jnp.sum(totals[k], 0, keepdims=True))
             behind = ahead
 
     first_rows(1)
@@ -247,7 +253,7 @@
     for b in range(CB):
         rows = slice(b * LANES, (b + 1) * LANES)
         total = jnp.sum(sp[rows, :].T, 0, keepdims=True)
-        gbuf[b:b + 1, :] = mbuf[b:b + 1, :] + jnp.log2(total)
+        gbuf[b:b + 1, :] = mbuf[b:b + 1, :] + ylow[b:b + 1, :] + jnp.log2(total)
 
     begin(to_column(gbuf, grec, gsend, grecv))
 
@@ -260,7 +266,7 @@
     lax.fori_loop(0, C // (4 * GROUP), halve, 0)
     all_of(grec, gsend, grecv).wait()
     lse = lse_of([gbuf[...]] + [grec[o] for o in range(S - 1)])
-    sig = jnp.exp2(mbuf[...] - lse)
+    sig = jnp.exp2(mbuf[...] + ylow[...] - lse)
     mbuf[...] = sig
     for b in range(CB):
         sb[b * LANES:(b + 1) * LANES, :] = turned(sig[b:b + 1, :])
@@ -460,7 +466,7 @@
         in_specs=[pl.BlockSpec(memory_space=pl.ANY)] + [whole] * 4,
         out_specs=(whole, whole),
         scratch_shapes=[
-            vmem((dims, R), F32), vmem((RB, LANES), F32), dma((R // min(512, R // 2),)),
+            vmem((dims, R), F32), vmem((RB, LANES), F32), vmem((CB, LANES), F32), dma((R // min(512, R // 2),)),
             vmem((4 * dims, R), BF16), vmem((C, 4 * dims), BF16), vmem((RB, C, LANES), F32),
             vmem((RB, C, LANES), BF16), vmem((RB, C, LANES), BF16), vmem((GROUP, R), F32),
             vmem((C, LANES), F32), vmem((C, LANES), F32), vmem((C, LANES), F32),

time: 52 us -> 51.9 us (level)
  no operation moved by 1% of the time
where the time goes in v5:
time: 51.9 us; the launch traced here: 51.8 us
  Pallas kernels  51.1 us (98%)
  between operations  0.64 us (1%)
    pallas_call x1, Pallas kernels, shards(): pl.pallas_call(functools.partial(kernel, S, T), out_shape=(vmem((dims, R...  50.4 us

profile of v5, /device:TPU:1, one launch (start us, length us, event | category | flops | bytes accessed | tf_op | source)
XLA Modules:
  0.0 51.8 jit_solution(4363049207615740888)
XLA Ops:
  0.6 50.4 %shard_map.68 = (f32[64,128]{1,0:T(8,128)S(1)}, f32[64,1024]{1,0:T(8,128)S(1)}) custom-call(f32[64,4096]{1,0:T(8,128)} %x_hbm.1, f32[64,1024]{1,0:T(8,128)} %y_ref.1, s32[1,4096]{1,0:T(1,128)} %bitcast.2, s32[1,1024]{1,0:T(1,128)} %bitcast.3, s32[64,64]{1,0:T(8,128)} %mask_ref.1), custom_call_target="tpu_custom_call" | custom-call | tf_op jit(solution)/shard_map/pallas_call | solution.py:463
  51.0 0.7 %shard_map.69 = (f32[64,128]{1,0:T(8,128)}, f32[64,1024]{1,0:T(8,128)}) custom-call(f32[64,128]{1,0:T(8,128)S(1)} %get-tuple-element.4.s_ref, f32[64,1024]{1,0:T(8,128)S(1)} %get-tuple-element.5.t_ref), custom_call_target="tpu_custom_call" | custom-call | tf_op jit(solution)/shard_map/pallas_call | solution.py:492

commit v6 on v4

--- a/solution.py
+++ b/solution.py
@@ -197,7 +197,7 @@
         for q in range(half_rows):
             frow[:, lanes_of(slot, q)] = jnp.broadcast_to(value[q:q + 1, :], (GROUP, LANES))
 
-    WIDE = 4
+    WIDE = 8
 
     def parts_of(value):
         return [value[g * GROUP:(g + 1) * GROUP] for g in range(value.shape[0] // GROUP)]
@@ -273,7 +273,9 @@
             weights = parts_of(sb[at, :])
             for q in range(half_rows):
                 terms = [z * w for z, w in zip(parts_of(zr[slot * half_rows + q, at, :]), weights)]
-                acc[q] = acc[q] + ((terms[0] + terms[1]) + (terms[2] + terms[3]))
+                while len(terms) > 1:
+                    terms = [u + v for u, v in zip(terms[::2], terms[1::2])]
+                acc[q] = acc[q] + terms[0]
             return tuple(acc)
 
         zero = jnp.zeros((GROUP, LANES), F32)

time: 52 us -> 51.6 us (level)
    pallas_call x1, Pallas kernels: 50.5 us -> 49.9 us  [shards(): pl.pallas_call(functools.partial(kernel, S, T), out_shape=(vmem((dims, R...]
where the time goes in v6:
time: 51.6 us; the launch traced here: 51.5 us
  Pallas kernels  50.7 us (98%)
  between operations  0.8 us (2%)
    pallas_call x1, Pallas kernels, shards(): pl.pallas_call(functools.partial(kernel, S, T), out_shape=(vmem((dims, R...  49.9 us

profile of v6, /device:TPU:1, one launch (start us, length us, event | category | flops | bytes accessed | tf_op | source)
XLA Modules:
  0.0 51.5 jit_solution(6246174685384721574)
XLA Ops:
  0.6 49.9 %shard_map.68 = (f32[64,128]{1,0:T(8,128)S(1)}, f32[64,1024]{1,0:T(8,128)S(1)}) custom-call(f32[64,4096]{1,0:T(8,128)} %x_hbm.1, f32[64,1024]{1,0:T(8,128)} %y_ref.1, s32[1,4096]{1,0:T(1,128)} %bitcast.2, s32[1,1024]{1,0:T(1,128)} %bitcast.3, s32[64,64]{1,0:T(8,128)} %mask_ref.1), custom_call_target="tpu_custom_call" | custom-call | tf_op jit(solution)/shard_map/pallas_call | solution.py:459
  50.6 0.7 %shard_map.69 = (f32[64,128]{1,0:T(8,128)}, f32[64,1024]{1,0:T(8,128)}) custom-call(f32[64,128]{1,0:T(8,128)S(1)} %get-tuple-element.4.s_ref, f32[64,1024]{1,0:T(8,128)S(1)} %get-tuple-element.5.t_ref), custom_call_target="tpu_custom_call" | custom-call | tf_op jit(solution)/shard_map/pallas_call | solution.py:488
